TPU v7x, 32 devices: a whole 2x2x4 slice. The times are simulated.
32 devices in a mesh: row: 8 (over y, x, core), col: 4 (over z).
Axes of the slice: x: 2, y: 2, z: 4, core: 2. Of those that a mesh axis runs over, the one named last changes fastest.
Arguments:
- features: bfloat16 [65536, 256], P(('col', 'row')), may hold values from -6 to 6
- block_values: bfloat16 [8, 4, 192, 128, 128], P('row', 'col'), may hold values from -0.1875 to 0.1875
- row_ptr: int32 [8, 4, 65], P('row', 'col'), may hold values from 0 to 144, as said below
- block_cols: int32 [8, 4, 192], P('row', 'col'), may hold values from 0 to 511, as said below
Outputs:
- product: bfloat16 [65536, 256], P(('row', 'col'))
Inputs may be any that keep to these rules, and one draw needn't show every extreme that they name: row_ptr[r, c, 0] = 0, row_ptr never falls along its last dimension, row_ptr[r, c, 64] <= 144, and on exactly one device row_ptr[r, c, 64] = 144. block_cols[r, c, s] lies in c * 128 to (c + 1) * 128 - 1; a block column may repeat within a block row, and repeated blocks add.
All inputs are finite; a program needn't handle non-finite values.
Results may differ from a plain program's by a relative error of at most 0.001.
Values may be sent and summed in bfloat16 or wider, within the bound.
A program may use at most 128 MiB of HBM per device.

v0:
```python
import functools

import jax
import jax.numpy as jnp
from jax import lax
from jax.experimental import pallas as pl
from jax.experimental.pallas import tpu as pltpu
from jax.sharding import PartitionSpec as P

LANES = 128
TOP = 32767.0
RIGHT, LEFT = 0, 1


def kernel(
    n_row, n_col, pointers, block_cols, features, values_hbm, out,
    panels, values, keep, sums, send_q, recv_q, send_s, recv_s,
    local_sem, ag_send, ag_recv, pair_send, pair_recv, rs_send, rs_recv, sc_send, sc_recv,
):
    n_chips = n_row // 2
    own_blocks = features.shape[0]
    half = own_blocks // 2
    chunks = len(panels)
    live = values.shape[0]
    shard = out.shape[0]
    parts, width = send_s.shape[3], send_s.shape[4]
    r, c = lax.axis_index("row"), lax.axis_index("col")
    chip, core = r // 2, r % 2
    square = n_chips == 4
    first_block = c * (own_blocks * n_row)

    def chip_to(o):
        if square:
            y, x = chip // 2, chip % 2
            return (1 - y if o >= 2 else y) * 2 + (1 - x if o % 2 else x)
        return (chip + o) % n_chips

    def chip_from(o):
        return chip_to(o) if square else (chip + n_chips - o) % n_chips

    partner = chip * 2 + 1 - core
    direct = (1, 2) if square else tuple(range(1, n_chips))

    def slot(k, row, h):
        return panels[k].at[pl.ds(row * own_blocks + h * half, half)]

    own = [
        pltpu.make_async_copy(
            features.at[:, :, pl.ds(k * LANES, LANES)],
            panels[k].at[pl.ds(r * own_blocks, own_blocks)],
            local_sem.at[k],
        )
        for k in range(chunks)
    ]
    for copy in own:
        copy.start()
    fetch = pltpu.make_async_copy(
        values_hbm.at[0, 0, pl.ds(0, live)], values, local_sem.at[chunks]
    )
    fetch.start()

    barrier = pltpu.get_barrier_semaphore()

    def greet(**where):
        pl.semaphore_signal(
            barrier, inc=1, device_id=where, device_id_type=pl.DeviceIdType.MESH
        )

    for o in direct:
        greet(row=chip_to(o) * 2 + core)
    greet(row=partner)
    pl.when(c > 0)(lambda: greet(col=c - 1))
    pl.when(c < n_col - 1)(lambda: greet(col=c + 1))
    ends = jnp.where(c > 0, 1, 0) + jnp.where(c < n_col - 1, 1, 0)
    pl.semaphore_wait(barrier, len(direct) + 1 + ends)

    def remote(src, dst, send, recv, **where):
        return pltpu.make_async_remote_copy(
            src_ref=src, dst_ref=dst, send_sem=send, recv_sem=recv,
            device_id=where, device_id_type=pl.DeviceIdType.MESH,
        )

    def piece(k, o, h, source, to):
        return remote(
            slot(k, source * 2 + core, h), slot(k, source * 2 + core, h),
            ag_send.at[k, o, h], ag_recv.at[k, o, h], row=to * 2 + core,
        )

    def across(k, o, h):
        return piece(k, o, h, chip, chip_to(o))

    def arriving(k, o, h):
        return piece(k, o, h, chip_from(o), chip_from(o))

    def relay(k, h):
        return piece(k, 3, h, chip_from(1 + h), chip_to(2 - h))

    def pair(k, o, h, whose):
        row = (chip_from(o) if o else chip) * 2 + whose
        return remote(
            slot(k, row, h), slot(k, row, h), pair_send.at[k, o, h], pair_recv.at[k, o, h],
            row=partner,
        )

    if square:
        order = ((1, 0), (2, 1), (1, 1), (2, 0))
    else:
        order = tuple((o, h) for o in direct for h in range(2))

    def gather_start(k):
        own[k].wait()
        for o, h in order:
            across(k, o, h).start()
        for h in range(2):
            pair(k, 0, h, core).start()

    def gather_finish(k):
        for o, h in order:
            arriving(k, o, h).wait_recv()
            if square and (o, h) in ((1, 0), (2, 1)):
                relay(k, h).start()
            pair(k, o, h, core).start()
        if square:
            for h in range(2):
                arriving(k, 3, h).wait_recv()
                pair(k, 3, h, core).start()
        for o in range(n_chips):
            for h in range(2):
                pair(k, o, h, 1 - core).wait_recv()

    unroll = 4 if live % 4 == 0 else 1

    def mark_rows():
        ids = lax.broadcasted_iota(jnp.int32, keep.shape, 0)

        def mark(q, flags):
            return jnp.where(ids == pointers[0, 0, q], 0.0, flags)

        keep[...] = lax.fori_loop(0, pointers.shape[2], mark, jnp.ones(keep.shape, jnp.float32))

    def compute(k):
        def step(i, total):
            first = i * unroll
            products = [
                jnp.dot(
                    values[first + u], panels[k][jnp.maximum(block_cols[0, 0, first + u] - first_block, 0)],
                    preferred_element_type=jnp.float32,
                )
                for u in range(unroll)
            ]
            for u in range(unroll):
                total = total * keep[pl.ds(first + u, 1), :] + products[u]
                sums[k, first + u] = total
            return total

        lax.fori_loop(0, live // unroll, step, jnp.zeros(sums.shape[2:], jnp.float32))

    def row_sum(k, q):
        begin, end = pointers[0, 0, q], pointers[0, 0, q + 1]
        return sums[k, jnp.maximum(end - 1, 0)] * jnp.where(end > begin, 1.0, 0.0)

    def received(way, k, j, s, b):
        levels = recv_q[way, k, j, s * width + b].astype(jnp.int32).astype(jnp.float32)
        return levels * recv_s[way, k, j, s, pl.ds(b, 1), :]

    def message(way, k, j, s):
        to = c + 1 if way == RIGHT else c - 1
        rows = pl.ds(s * width, width)
        return (
            remote(send_q.at[way, k, j, rows], recv_q.at[way, k, j, rows],
                   rs_send.at[way, k, j, s], rs_recv.at[way, k, j, s], col=to),
            remote(send_s.at[way, k, j, s], recv_s.at[way, k, j, s],
                   sc_send.at[way, k, j, s], sc_recv.at[way, k, j, s], col=to),
        )

    def forward(way, k, j, s, incoming):
        if incoming:
            for copy in message(way, k, j, s):
                copy.wait_recv()

        def one(b, carry):
            x = row_sum(k, j * shard + s * width + b)
            if incoming:
                x = x + received(way, k, j, s, b)
            most = jnp.maximum(jnp.max(jnp.abs(x), axis=0, keepdims=True), 1e-30)
            send_s[way, k, j, s, pl.ds(b, 1), :] = most * (1.0 / TOP)
            levels = jnp.round(x * (TOP / most)).astype(jnp.int32)
            send_q[way, k, j, s * width + b] = levels.astype(jnp.int16)
            return carry

        lax.fori_loop(0, width, one, 0)
        for copy in message(way, k, j, s):
            copy.start()

    def scatter_ends(k):
        def right(m, carry):
            forward(RIGHT, k, n_col - 1 - m // parts, m % parts, False)
            return carry

        def left(m, carry):
            forward(LEFT, k, m // parts, m % parts, False)
            return carry

        total = (n_col - 1) * parts

        @pl.when(c == 0)
        def _():
            lax.fori_loop(0, total, right, 0)

        @pl.when(c == n_col - 1)
        def _():
            lax.fori_loop(0, total, left, 0)

    def scatter_middle(k):
        def unit(n, carry):
            right = n - c
            left = n - (n_col - 1 - c)

            @pl.when((c > 0) & (right >= 0) & (right < (n_col - 1 - c) * parts))
            def _():
                forward(RIGHT, k, n_col - 1 - right // parts, right % parts, True)

            @pl.when((c < n_col - 1) & (left >= 0) & (left < c * parts))
            def _():
                forward(LEFT, k, left // parts, left % parts, True)

            return carry

        lax.fori_loop(1, (n_col - 2) * parts + 1, unit, 0)

    def finish(k):
        def write(ways):
            def part(s, carry):
                for way in ways:
                    for copy in message(way, k, c, s):
                        copy.wait_recv()

                def one(b, inner):
                    x = row_sum(k, c * shard + s * width + b)
                    for way in ways:
                        x = x + received(way, k, c, s, b)
                    out[s * width + b, :, pl.ds(k * LANES, LANES)] = x.astype(out.dtype)
                    return inner

                return lax.fori_loop(0, width, one, carry)

            lax.fori_loop(0, parts, part, 0)

        pl.when(c == 0)(lambda: write((LEFT,)))
        pl.when(c == n_col - 1)(lambda: write((RIGHT,)))
        pl.when((c > 0) & (c < n_col - 1))(lambda: write((RIGHT, LEFT)))

    gather_start(0)
    mark_rows()
    fetch.wait()
    gather_finish(0)
    for k in range(chunks):
        if k + 1 < chunks:
            gather_start(k + 1)
        compute(k)
        scatter_ends(k)
        if k > 0:
            scatter_middle(k - 1)
            finish(k - 1)
        if k + 1 < chunks:
            gather_finish(k + 1)
    scatter_middle(chunks - 1)
    finish(chunks - 1)

    for k in range(chunks):
        for h in range(2):
            for o in direct:
                across(k, o, h).wait_send()
            if square:
                relay(k, h).wait_send()
            for o in range(n_chips):
                pair(k, o, h, core).wait_send()
        for way in (RIGHT, LEFT):
            def drain(m, carry, way=way, k=k):
                j = m // parts

                @pl.when((j > c) if way == RIGHT else (j < c))
                def _():
                    for copy in message(way, k, j, m % parts):
                        copy.wait_send()

                return carry

            lax.fori_loop(0, n_col * parts, drain, 0)


def local(n_row, n_col, features, block_values, row_ptr, block_cols):
    slots, block = block_values.shape[2], block_values.shape[3]
    live = slots * 3 // 4
    own_blocks = features.shape[0] // block
    group_blocks = own_blocks * n_row
    chunks = features.shape[1] // LANES
    shard = (row_ptr.shape[2] - 1) // n_col
    parts = 4 if shard % 4 == 0 else 1
    smem = pl.BlockSpec(memory_space=pltpu.SMEM)
    hbm = pl.BlockSpec(memory_space=pl.ANY)
    messages = (2, chunks, n_col)
    gathers = (chunks, n_row // 2, 2)
    result = pl.pallas_call(
        functools.partial(kernel, n_row, n_col),
        out_shape=jax.ShapeDtypeStruct((shard, block, features.shape[1]), jnp.bfloat16),
        in_specs=[smem] * 2 + [hbm] * 2,
        out_specs=pl.BlockSpec(memory_space=pltpu.VMEM),
        scratch_shapes=[
            [pltpu.VMEM((group_blocks, block, LANES), jnp.bfloat16)] * chunks,
            pltpu.VMEM((live, block, block), jnp.bfloat16),
            pltpu.VMEM((live, LANES), jnp.float32),
            pltpu.VMEM((chunks, live, block, LANES), jnp.float32),
            pltpu.VMEM(messages + (shard, block, LANES), jnp.int16),
            pltpu.VMEM(messages + (shard, block, LANES), jnp.int16),
            pltpu.VMEM(messages + (parts, shard // parts, LANES), jnp.float32),
            pltpu.VMEM(messages + (parts, shard // parts, LANES), jnp.float32),
            pltpu.SemaphoreType.DMA((chunks + 1,)),
        ]
        + [pltpu.SemaphoreType.DMA(gathers)] * 4
        + [pltpu.SemaphoreType.DMA(messages + (parts,))] * 4,
        compiler_params=pltpu.CompilerParams(
            collective_id=0, has_side_effects=True, vmem_limit_bytes=67043328
        ),
    )(row_ptr, block_cols, features.reshape(own_blocks, block, -1), block_values)
    return result.reshape(shard * block, -1)


def solution(mesh):
    return jax.shard_map(
        functools.partial(local, mesh.shape["row"], mesh.shape["col"]),
        mesh=mesh,
        in_specs=(
            P(("col", "row"), None),
            P("row", "col", None, None, None),
            P("row", "col", None),
            P("row", "col", None),
        ),
        out_specs=P(("row", "col"), None),
        check_vma=False,
    )
```

profile of v0, /device:TPU:8, one launch (start us, length us, event | category | flops | bytes accessed | tf_op | source)
XLA Modules:
  0.0 108.7 jit_solution(317353132084701581)
XLA Ops:
  0.0 106.4 %shard_map.46 = bf16[16,128,256]{2,1,0:T(8,128)(2,1)} custom-call(s32[1,1,65]{2,1,0:T(1,128)} %pointers.1, s32[1,1,192]{2,1,0:T(1,128)} %block_cols.1, bf16[16,128,256]{2,1,0:T(8,128)(2,1)} %bitcast.3, bf16[1,1,192,128,128]{4,3,2,1,0:T(8,128)(2,1)} %values_hbm.1), custom_call_target="tpu_custom_call" | custom-call | tf_op jit(solution)/shard_map/pallas_call | solution.py:304
  106.4 2.3 %copy.6 = bf16[2048,256]{1,0:T(8,128)(2,1)} copy(bf16[2048,256]{1,0:T(8,128)(2,1)} %bitcast.2) | data formatting | bytes 2097152
where the time goes:
time: 109 us
  Pallas kernels  106 us (97%)
  local copies, waits for them, and re-layouts  2.26 us (2%)
    pallas_call x1, Pallas kernels, local(): pl.pallas_call(functools.partial(kernel, n_row, n_col), out_shape=jax.Sha...  106 us
    unnamed x1, local copies, waits for them, and re-layouts  2.26 us

commit v1 on v0

v1 whole, which is shorter than its diff:
```python
import functools

import jax
import jax.numpy as jnp
from jax import lax
from jax.experimental import pallas as pl
from jax.experimental.pallas import tpu as pltpu
from jax.sharding import PartitionSpec as P

LANES = 128
TOP = 32767.0
RIGHT, LEFT = 0, 1


def column_chunks(columns):
    chunks = [(0, 32), (32, 32), (64, 64)]
    for first in range(LANES, columns, 64):
        chunks.append((first, 64))
    return chunks


def parts_of(width, shard):
    parts = {32: 2, 64: 4, 128: 4}[width]
    while shard % parts:
        parts //= 2
    return parts


def kernel(
    n_row, n_col, pieces,
    pointers, block_cols, features, values_hbm, out,
    stage, panels, values, keep, sums, rows, tops, send_q, recv_q, send_s, recv_s,
    local_sem, ag_send, ag_recv, pair_send, pair_recv, rs_send, rs_recv, sc_send, sc_recv,
):
    n_chips = n_row // 2
    own_blocks = features.shape[0]
    block = features.shape[1]
    square = n_chips == 4
    halves = 2 if square else 1
    half = own_blocks // halves
    chunks = len(panels)
    live = values.shape[0]
    shard = out.shape[0]
    tiles = features.shape[2] // LANES
    r, c = lax.axis_index("row"), lax.axis_index("col")
    chip, core = r // 2, r % 2
    first_block = c * (own_blocks * n_row)
    parts = [p.shape[1] for p in tops]
    depth = [p.shape[1] for p in panels]
    fold = [block // d for d in depth]

    def chip_to(o):
        if square:
            y, x = chip // 2, chip % 2
            return (1 - y if o >= 2 else y) * 2 + (1 - x if o % 2 else x)
        return (chip + o) % n_chips

    def chip_from(o):
        return chip_to(o) if square else (chip + n_chips - o) % n_chips

    partner = chip * 2 + 1 - core
    direct = (1, 2) if square else tuple(range(1, n_chips))

    def slot(k, row, h):
        return panels[k].at[pl.ds(row * own_blocks + h * half, half)]

    own = [
        pltpu.make_async_copy(
            features.at[:, :, pl.ds(t * LANES, LANES)], stage.at[t], local_sem.at[t]
        )
        for t in range(tiles)
    ]
    for copy in own:
        copy.start()
    fetch = pltpu.make_async_copy(
        values_hbm.at[0, 0, pl.ds(0, live)], values, local_sem.at[tiles]
    )
    fetch.start()

    barrier = pltpu.get_barrier_semaphore()

    def greet(**where):
        pl.semaphore_signal(
            barrier, inc=1, device_id=where, device_id_type=pl.DeviceIdType.MESH
        )

    for o in direct:
        greet(row=chip_to(o) * 2 + core)
    greet(row=partner)
    pl.when(c > 0)(lambda: greet(col=c - 1))
    pl.when(c < n_col - 1)(lambda: greet(col=c + 1))

    lane = lax.broadcasted_iota(jnp.int32, (1, LANES), 1)

    def pack_own(k):
        first, width = pieces[k]
        tile, offset = first // LANES, first % LANES
        d, f = depth[k], fold[k]

        def one(b, carry):
            packed = None
            for m in range(f):
                x = stage[tile, b, pl.ds(m * d, d), :].astype(jnp.float32)
                x = pltpu.roll(x, (m * width - offset) % LANES, 1)
                packed = x if m == 0 else jnp.where(lane >= m * width, x, packed)
            panels[k][r * own_blocks + b] = packed.astype(jnp.bfloat16)
            return carry

        lax.fori_loop(0, own_blocks, one, 0)

    def remote(src, dst, send, recv, **where):
        return pltpu.make_async_remote_copy(
            src_ref=src, dst_ref=dst, send_sem=send, recv_sem=recv,
            device_id=where, device_id_type=pl.DeviceIdType.MESH,
        )

    def piece(k, o, h, source, to):
        return remote(
            slot(k, source * 2 + core, h), slot(k, source * 2 + core, h),
            ag_send.at[k, o, h], ag_recv.at[k, o, h], row=to * 2 + core,
        )

    def across(k, o, h):
        return piece(k, o, h, chip, chip_to(o))

    def arriving(k, o, h):
        return piece(k, o, h, chip_from(o), chip_from(o))

    def relay(k, h):
        return piece(k, 3, h, chip_from(1 + h), chip_to(2 - h))

    def pair(k, o, h, whose):
        row = (chip_from(o) if o else chip) * 2 + whose
        return remote(
            slot(k, row, h), slot(k, row, h), pair_send.at[k, o, h], pair_recv.at[k, o, h],
            row=partner,
        )

    if square:
        order = ((1, 0), (2, 1), (1, 1), (2, 0))
    else:
        order = tuple((o, 0) for o in direct)

    def gather_start(k):
        for o, h in order:
            across(k, o, h).start()
        for h in range(halves):
            pair(k, 0, h, core).start()

    def gather_relay(k):
        for o, h in order:
            arriving(k, o, h).wait_recv()
            if square and (o, h) in ((1, 0), (2, 1)):
                relay(k, h).start()
            pair(k, o, h, core).start()

    def gather_finish(k):
        if square:
            for h in range(halves):
                arriving(k, 3, h).wait_recv()
                pair(k, 3, h, core).start()
        for o in range(n_chips):
            for h in range(halves):
                pair(k, o, h, 1 - core).wait_recv()

    unroll = 1
    for u in (2, 4, 8, 16):
        if live % u == 0:
            unroll = u

    def mark_rows():
        ids = lax.broadcasted_iota(jnp.int32, keep.shape, 0)

        def mark(q, flags):
            return jnp.where(ids == pointers[0, 0, q], 0.0, flags)

        keep[...] = lax.fori_loop(0, pointers.shape[2], mark, jnp.ones(keep.shape, jnp.float32))

    def compute(k):
        width = pieces[k][1]

        def panel(s):
            x = panels[k][jnp.maximum(block_cols[0, 0, s] - first_block, 0)]
            if fold[k] == 1:
                return x
            turned = [x] + [pltpu.roll(x, LANES - m * width, 1) for m in range(1, fold[k])]
            return jnp.concatenate(turned, axis=0)

        def step(i, total):
            first = i * unroll
            products = [
                jnp.dot(values[first + u], panel(first + u), preferred_element_type=jnp.float32)
                for u in range(unroll)
            ]
            for u in range(unroll):
                total = total * keep[pl.ds(first + u, 1), :] + products[u]
                sums[first + u] = total
            return total

        lax.fori_loop(0, live // unroll, step, jnp.zeros(sums.shape[1:], jnp.float32))

    def row_sum(k, q):
        width, d = pieces[k][1], depth[k]
        begin, end = pointers[0, 0, q], pointers[0, 0, q + 1]
        last = jnp.maximum(end - 1, 0)
        packed = None
        for m in range(fold[k]):
            x = sums[last, pl.ds(m * d, d), :]
            if m == 0:
                packed = x
            else:
                packed = jnp.where(lane >= m * width, pltpu.roll(x, m * width, 1), packed)
        return packed * jnp.where(end > begin, 1.0, 0.0)

    def collect(k, j, s):
        width = shard // parts[k]

        def one(b, top):
            q = j * shard + s * width + b
            x = row_sum(k, q)
            rows[k][q] = x
            return jnp.maximum(top, jnp.max(jnp.abs(x).reshape(-1, 8, LANES), axis=0))

        top = lax.fori_loop(0, width, one, jnp.zeros((8, LANES), jnp.float32))
        tops[k][j, s] = jnp.max(top, axis=0, keepdims=True)

    def seat(way, j):
        return j + 1 if way == RIGHT else j

    def received(way, k, j, s, b):
        width = shard // parts[k]
        levels = recv_q[k][seat(way, j), s * width + b].astype(jnp.int32).astype(jnp.float32)
        return levels * recv_s[k][seat(way, j), s]

    def message(way, k, j, s):
        width = shard // parts[k]
        to = c + 1 if way == RIGHT else c - 1
        span = pl.ds(s * width, width)
        there = seat(way, j)
        return (
            remote(send_q[k].at[j, span], recv_q[k].at[there, span],
                   rs_send[k].at[j, s], rs_recv[k].at[there, s], col=to),
            remote(send_s[k].at[j, s], recv_s[k].at[there, s],
                   sc_send[k].at[j, s], sc_recv[k].at[there, s], col=to),
        )

    def forward(way, k, j, s, incoming):
        width = shard // parts[k]
        most = tops[k][j, s]
        if incoming:
            for copy in message(way, k, j, s):
                copy.wait_recv()
            most = most + recv_s[k][seat(way, j), s] * TOP
        most = jnp.maximum(most, 1e-30)
        send_s[k][j, s] = most * (1.0 / TOP)
        gain = TOP / most

        def one(b, carry):
            x = rows[k][j * shard + s * width + b]
            if incoming:
                x = x + received(way, k, j, s, b)
            send_q[k][j, s * width + b] = jnp.round(x * gain).astype(jnp.int32).astype(jnp.int16)
            return carry

        lax.fori_loop(0, width, one, 0)
        for copy in message(way, k, j, s):
            copy.start()

    def scatter_start(k):
        n = parts[k]

        def right(m, carry):
            collect(k, n_col - 1 - m // n, m % n)
            forward(RIGHT, k, n_col - 1 - m // n, m % n, False)
            return carry

        def left(m, carry):
            collect(k, m // n, m % n)
            forward(LEFT, k, m // n, m % n, False)
            return carry

        def keep_own(m, carry):
            collect(k, c, m)
            return carry

        def keep_all(m, carry):
            collect(k, m // n, m % n)
            return carry

        total = (n_col - 1) * n

        @pl.when(c == 0)
        def _():
            lax.fori_loop(0, total, right, 0)
            lax.fori_loop(0, n, keep_own, 0)

        @pl.when(c == n_col - 1)
        def _():
            lax.fori_loop(0, total, left, 0)
            lax.fori_loop(0, n, keep_own, 0)

        @pl.when((c > 0) & (c < n_col - 1))
        def _():
            lax.fori_loop(0, n_col * n, keep_all, 0)

    def scatter_middle(k):
        p = parts[k]

        def unit(n, carry):
            right = n - c
            left = n - (n_col - 1 - c)

            @pl.when((c > 0) & (right >= 0) & (right < (n_col - 1 - c) * p))
            def _():
                forward(RIGHT, k, n_col - 1 - right // p, right % p, True)

            @pl.when((c < n_col - 1) & (left >= 0) & (left < c * p))
            def _():
                forward(LEFT, k, left // p, left % p, True)

            return carry

        lax.fori_loop(1, (n_col - 2) * p + 1, unit, 0)

    def finish(k):
        first, columns = pieces[k]
        tile, offset = first // LANES, first % LANES
        width = shard // parts[k]
        d = depth[k]

        def write(ways):
            def part(s, carry):
                for way in ways:
                    for copy in message(way, k, c, s):
                        copy.wait_recv()

                def one(b, inner):
                    x = rows[k][c * shard + s * width + b]
                    for way in ways:
                        x = x + received(way, k, c, s, b)
                    for m in range(fold[k]):
                        y = pltpu.roll(x, (offset - m * columns) % LANES, 1)
                        out[s * width + b, pl.ds(m * d, d), pl.ds(first, columns)] = (
                            y[:, offset:offset + columns].astype(out.dtype)
                        )
                    return inner

                return lax.fori_loop(0, width, one, carry)

            lax.fori_loop(0, parts[k], part, 0)

        pl.when(c == 0)(lambda: write((LEFT,)))
        pl.when(c == n_col - 1)(lambda: write((RIGHT,)))
        pl.when((c > 0) & (c < n_col - 1))(lambda: write((RIGHT, LEFT)))

    own[0].wait()
    pack_own(0)
    ends = jnp.where(c > 0, 1, 0) + jnp.where(c < n_col - 1, 1, 0)
    pl.semaphore_wait(barrier, len(direct) + 1 + ends)
    gather_start(0)
    for copy in own[1:]:
        copy.wait()
    pack_own(1)
    mark_rows()
    gather_relay(0)
    gather_start(1)
    for k in range(2, chunks):
        pack_own(k)
    fetch.wait()
    gather_finish(0)
    for k in range(chunks):
        compute(k)
        scatter_start(k)
        if k + 1 < chunks:
            gather_relay(k + 1)
        if k + 2 < chunks:
            gather_start(k + 2)
        if k > 0:
            scatter_middle(k - 1)
            finish(k - 1)
        if k + 1 < chunks:
            gather_finish(k + 1)
    scatter_middle(chunks - 1)
    finish(chunks - 1)

    for k in range(chunks):
        for h in range(halves):
            for o in direct:
                across(k, o, h).wait_send()
            if square:
                relay(k, h).wait_send()
            for o in range(n_chips):
                pair(k, o, h, core).wait_send()
        for way in (RIGHT, LEFT):
            def drain(m, carry, way=way, k=k):
                j = m // parts[k]

                @pl.when((j > c) if way == RIGHT else (j < c))
                def _():
                    for copy in message(way, k, j, m % parts[k]):
                        copy.wait_send()

                return carry

            lax.fori_loop(0, n_col * parts[k], drain, 0)


def local(n_row, n_col, features, block_values, row_ptr, block_cols):
    slots, block = block_values.shape[2], block_values.shape[3]
    live = slots * 3 // 4
    own_blocks = features.shape[0] // block
    group_blocks = own_blocks * n_row
    columns = features.shape[1]
    pieces = column_chunks(columns)
    shard = (row_ptr.shape[2] - 1) // n_col
    parts = [parts_of(width, shard) for _, width in pieces]
    depth = [block * width // LANES for _, width in pieces]
    smem = pl.BlockSpec(memory_space=pltpu.SMEM)
    hbm = pl.BlockSpec(memory_space=pl.ANY)
    halves = 2 if n_row == 8 else 1
    gathers = (len(pieces), n_row // 2, halves)

    def per_chunk(make):
        return [make(p, d) for p, d in zip(parts, depth)]

    dma = pltpu.SemaphoreType.DMA
    result = pl.pallas_call(
        functools.partial(kernel, n_row, n_col, pieces),
        out_shape=jax.ShapeDtypeStruct((shard, block, columns), jnp.bfloat16),
        in_specs=[smem] * 2 + [hbm] * 2,
        out_specs=pl.BlockSpec(memory_space=pltpu.VMEM),
        scratch_shapes=[
            pltpu.VMEM((columns // LANES, own_blocks, block, LANES), jnp.bfloat16),
            per_chunk(lambda p, d: pltpu.VMEM((group_blocks, d, LANES), jnp.bfloat16)),
            pltpu.VMEM((live, block, block), jnp.bfloat16),
            pltpu.VMEM((live, LANES), jnp.float32),
            pltpu.VMEM((live, block, LANES), jnp.float32),
            per_chunk(lambda p, d: pltpu.VMEM((shard * n_col, d, LANES), jnp.float32)),
            per_chunk(lambda p, d: pltpu.VMEM((n_col, p, 1, LANES), jnp.float32)),
            per_chunk(lambda p, d: pltpu.VMEM((n_col, shard, d, LANES), jnp.int16)),
            per_chunk(lambda p, d: pltpu.VMEM((n_col + 1, shard, d, LANES), jnp.int16)),
            per_chunk(lambda p, d: pltpu.VMEM((n_col, p, 1, LANES), jnp.float32)),
            per_chunk(lambda p, d: pltpu.VMEM((n_col + 1, p, 1, LANES), jnp.float32)),
            dma((columns // LANES + 1,)),
        ]
        + [dma(gathers)] * 4
        + [
            per_chunk(lambda p, d: dma((n_col, p))),
            per_chunk(lambda p, d: dma((n_col + 1, p))),
            per_chunk(lambda p, d: dma((n_col, p))),
            per_chunk(lambda p, d: dma((n_col + 1, p))),
        ],
        compiler_params=pltpu.CompilerParams(
            collective_id=0, has_side_effects=True, vmem_limit_bytes=67043328
        ),
    )(row_ptr, block_cols, features.reshape(own_blocks, block, -1), block_values)
    return result.reshape(shard * block, -1)


def solution(mesh):
    return jax.shard_map(
        functools.partial(local, mesh.shape["row"], mesh.shape["col"]),
        mesh=mesh,
        in_specs=(
            P(("col", "row"), None),
            P("row", "col", None, None, None),
            P("row", "col", None),
            P("row", "col", None),
        ),
        out_specs=P(("row", "col"), None),
        check_vma=False,
    )
```

time: 109 us -> 149 us (1.37)
  Pallas kernels: 106 us -> 146 us
    pallas_call x1, Pallas kernels: 106 us -> 146 us  [local(): pl.pallas_call(functools.partial(kernel, n_row, n_col, pieces), out_shape...]
where the time goes in v1:
time: 149 us
  Pallas kernels  146 us (98%)
  local copies, waits for them, and re-layouts  2.26 us (2%)
    pallas_call x1, Pallas kernels, local(): pl.pallas_call(functools.partial(kernel, n_row, n_col, pieces), out_shape...  146 us

profile of v1, /device:TPU:8, one launch (start us, length us, event | category | flops | bytes accessed | tf_op | source)
XLA Modules:
  0.0 148.7 jit_solution(1257042578182679261)
XLA Ops:
  0.0 146.4 %shard_map.46 = bf16[16,128,256]{2,1,0:T(8,128)(2,1)} custom-call(s32[1,1,65]{2,1,0:T(1,128)} %pointers.1, s32[1,1,192]{2,1,0:T(1,128)} %block_cols.1, bf16[16,128,256]{2,1,0:T(8,128)(2,1)} %bitcast.3, bf16[1,1,192,128,128]{4,3,2,1,0:T(8,128)(2,1)} %values_hbm.1), custom_call_target="tpu_custom_call" | custom-call | tf_op jit(solution)/shard_map/pallas_call | solution.py:427
  146.4 2.3 %copy.6 = bf16[2048,256]{1,0:T(8,128)(2,1)} copy(bf16[2048,256]{1,0:T(8,128)(2,1)} %bitcast.2) | data formatting | bytes 2097152

commit v2 on v1

v2 whole, which is shorter than its diff:
```python
import functools

import jax
import jax.numpy as jnp
from jax import lax
from jax.experimental import pallas as pl
from jax.experimental.pallas import tpu as pltpu
from jax.sharding import PartitionSpec as P

LANES = 128
TOP = 32767.0
RIGHT, LEFT = 0, 1


def column_chunks(columns):
    chunks = [(0, 32), (32, 32), (64, 64)]
    for first in range(LANES, columns, 64):
        chunks.append((first, 64))
    return chunks


def parts_of(width, shard):
    parts = {32: 1, 64: 2, 128: 4}[width]
    while shard % parts:
        parts //= 2
    return parts


def kernel(
    n_row, n_col, pieces,
    pointers_hbm, block_cols_hbm, features, values_hbm, out,
    pointers, block_cols, stage, panels, values, keep, sums, rows, tops, send_q, recv_q, send_s, recv_s,
    local_sem, table_sem, ag_send, ag_recv, pair_send, pair_recv, rs_send, rs_recv, sc_send, sc_recv,
):
    n_chips = n_row // 2
    own_blocks = features.shape[0]
    block = features.shape[1]
    square = n_chips == 4
    halves = 2 if square else 1
    half = own_blocks // halves
    chunks = len(panels)
    live = values.shape[0]
    shard = out.shape[0]
    tiles = features.shape[2] // LANES
    r, c = lax.axis_index("row"), lax.axis_index("col")
    chip, core = r // 2, r % 2
    first_block = c * (own_blocks * n_row)
    parts = [p.shape[1] for p in rs_recv]
    depth = [p.shape[1] for p in panels]
    fold = [block // d for d in depth]

    def chip_to(o):
        if square:
            y, x = chip // 2, chip % 2
            return (1 - y if o >= 2 else y) * 2 + (1 - x if o % 2 else x)
        return (chip + o) % n_chips

    def chip_from(o):
        return chip_to(o) if square else (chip + n_chips - o) % n_chips

    partner = chip * 2 + 1 - core
    direct = (1, 2) if square else tuple(range(1, n_chips))

    def slot(k, row, h):
        return panels[k].at[pl.ds(row * own_blocks + h * half, half)]

    own = [
        pltpu.make_async_copy(
            features.at[:, :, pl.ds(t * LANES, LANES)], stage.at[t], local_sem.at[t]
        )
        for t in range(tiles)
    ]
    for copy in own:
        copy.start()
    tables = [
        pltpu.make_async_copy(pointers_hbm, pointers, table_sem.at[0]),
        pltpu.make_async_copy(block_cols_hbm, block_cols, table_sem.at[1]),
    ]
    for copy in tables:
        copy.start()
    fetch = pltpu.make_async_copy(
        values_hbm.at[0, 0, pl.ds(0, live)], values, local_sem.at[tiles]
    )
    fetch.start()

    barrier = pltpu.get_barrier_semaphore()

    def greet(**where):
        pl.semaphore_signal(
            barrier, inc=1, device_id=where, device_id_type=pl.DeviceIdType.MESH
        )

    for o in direct:
        greet(row=chip_to(o) * 2 + core)
    greet(row=partner)
    pl.when(c > 0)(lambda: greet(col=c - 1))
    pl.when(c < n_col - 1)(lambda: greet(col=c + 1))

    lane = lax.broadcasted_iota(jnp.int32, (1, LANES), 1)

    def each(count, batch, body):
        while count % batch:
            batch //= 2

        def step(i, carry):
            body([i * batch + u for u in range(batch)])
            return carry

        lax.fori_loop(0, count // batch, step, 0)

    def pack_own(k):
        first, width = pieces[k]
        tile, offset = first // LANES, first % LANES
        d, f = depth[k], fold[k]

        def one(b):
            packed = None
            for m in range(f):
                x = stage[tile, b, pl.ds(m * d, d), :].astype(jnp.float32)
                x = pltpu.roll(x, (m * width - offset) % LANES, 1)
                packed = x if m == 0 else jnp.where(lane >= m * width, x, packed)
            return packed.astype(jnp.bfloat16)

        def some(blocks):
            for b, packed in [(b, one(b)) for b in blocks]:
                panels[k][r * own_blocks + b] = packed

        each(own_blocks, 4, some)

    def remote(src, dst, send, recv, **where):
        return pltpu.make_async_remote_copy(
            src_ref=src, dst_ref=dst, send_sem=send, recv_sem=recv,
            device_id=where, device_id_type=pl.DeviceIdType.MESH,
        )

    def piece(k, o, h, source, to):
        return remote(
            slot(k, source * 2 + core, h), slot(k, source * 2 + core, h),
            ag_send.at[k], ag_recv.at[k, o, h], row=to * 2 + core,
        )

    def across(k, o, h):
        return piece(k, o, h, chip, chip_to(o))

    def arriving(k, o, h):
        return piece(k, o, h, chip_from(o), chip_from(o))

    def relay(k, h):
        return piece(k, 3, h, chip_from(1 + h), chip_to(2 - h))

    def pair(k, o, h, whose):
        row = (chip_from(o) if o else chip) * 2 + whose
        return remote(
            slot(k, row, h), slot(k, row, h), pair_send.at[k], pair_recv.at[k], row=partner,
        )

    def gathered(k, count, sent):
        span = panels[k].at[pl.ds(0, count * own_blocks)]
        return remote(span, span, sent.at[k], pair_recv.at[k], row=partner)

    if square:
        order = ((1, 0), (2, 1), (1, 1), (2, 0))
    else:
        order = tuple((o, 0) for o in direct)

    def gather_start(k):
        for o, h in order:
            across(k, o, h).start()
        for h in range(halves):
            pair(k, 0, h, core).start()

    def gather_relay(k):
        for o, h in order:
            arriving(k, o, h).wait_recv()
            if square and (o, h) in ((1, 0), (2, 1)):
                relay(k, h).start()
            pair(k, o, h, core).start()

    def gather_finish(k):
        if square:
            for h in range(halves):
                arriving(k, 3, h).wait_recv()
                pair(k, 3, h, core).start()
        gathered(k, n_chips, pair_send).wait_recv()

    unroll = 1
    for u in (2, 4, 8, 16):
        if live % u == 0:
            unroll = u

    def mark_rows():
        ids = lax.broadcasted_iota(jnp.int32, keep.shape, 0)

        def mark(q, flags):
            return jnp.where(ids == pointers[0, 0, q], 0.0, flags)

        keep[...] = lax.fori_loop(0, pointers.shape[2], mark, jnp.ones(keep.shape, jnp.float32))

    def compute(k, between=None):
        width = pieces[k][1]

        def panel(s):
            x = panels[k][jnp.maximum(block_cols[0, 0, s] - first_block, 0)]
            if fold[k] == 1:
                return x
            turned = [x] + [pltpu.roll(x, LANES - m * width, 1) for m in range(1, fold[k])]
            return jnp.concatenate(turned, axis=0)

        def step(i, total):
            first = i * unroll
            products = [
                jnp.dot(values[first + u], panel(first + u), preferred_element_type=jnp.float32)
                for u in range(unroll)
            ]
            for u in range(unroll):
                total = total * keep[pl.ds(first + u, 1), :] + products[u]
                sums[first + u] = total
            return total

        steps = live // unroll
        total = jnp.zeros(sums.shape[1:], jnp.float32)
        if between is not None:
            total = lax.fori_loop(0, steps // 2, step, total)
            between()
            lax.fori_loop(steps // 2, steps, step, total)
        else:
            lax.fori_loop(0, steps, step, total)

    def row_sum(k, q):
        width, d = pieces[k][1], depth[k]
        begin, end = pointers[0, 0, q], pointers[0, 0, q + 1]
        last = jnp.maximum(end - 1, 0)
        packed = None
        for m in range(fold[k]):
            x = sums[last, pl.ds(m * d, d), :]
            if m == 0:
                packed = x
            else:
                packed = jnp.where(lane >= m * width, pltpu.roll(x, m * width, 1), packed)
        return packed * jnp.where(end > begin, 1.0, 0.0)

    def collect(k, j):
        width = shard // parts[k]

        def part(s, top):
            first = j * shard + s * width
            found = [row_sum(k, first + b) for b in range(width)]
            for b, x in enumerate(found):
                rows[k][first + b] = x
            for x in found:
                top = jnp.maximum(top, jnp.max(jnp.abs(x).reshape(-1, 8, LANES), axis=0))
            return top

        top = lax.fori_loop(0, parts[k], part, jnp.zeros((8, LANES), jnp.float32))
        tops[k][j] = jnp.max(top, axis=0, keepdims=True)

    def seat(way, j):
        return j + 1 if way == RIGHT else j

    def received(way, k, j, s, b):
        width = shard // parts[k]
        levels = recv_q[k][seat(way, j), s * width + b].astype(jnp.int32).astype(jnp.float32)
        return levels * recv_s[k][seat(way, j)]

    def message(way, k, j, s):
        width = shard // parts[k]
        span = pl.ds(s * width, width)
        there = seat(way, j)
        return remote(
            send_q[k].at[j, span], recv_q[k].at[there, span], rs_send.at[k], rs_recv[k].at[there, s],
            col=c + 1 if way == RIGHT else c - 1,
        )

    def scale(way, k, j):
        there = seat(way, j)
        return remote(
            send_s[k].at[j], recv_s[k].at[there], sc_send.at[k], sc_recv.at[k, there],
            col=c + 1 if way == RIGHT else c - 1,
        )

    def announce(way, k, j, incoming):
        most = tops[k][j]
        if incoming:
            scale(way, k, j).wait_recv()
            most = most + recv_s[k][seat(way, j)] * TOP
        send_s[k][j] = jnp.maximum(most, 1e-30) * (1.0 / TOP)
        scale(way, k, j).start()

    def forward(way, k, j, s, incoming):
        width = shard // parts[k]
        if incoming:
            message(way, k, j, s).wait_recv()
        gain = 1.0 / send_s[k][j]

        def one(b):
            x = rows[k][j * shard + s * width + b]
            if incoming:
                x = x + received(way, k, j, s, b)
            return jnp.round(x * gain).astype(jnp.int32).astype(jnp.int16)

        for b, levels in [(b, one(b)) for b in range(width)]:
            send_q[k][j, s * width + b] = levels
        message(way, k, j, s).start()

    def scatter_start(k):
        def ship(way, j):
            collect(k, j)
            announce(way, k, j, False)

            def part(s, carry):
                forward(way, k, j, s, False)
                return carry

            lax.fori_loop(0, parts[k], part, 0)

        def right(m, carry):
            ship(RIGHT, n_col - 1 - m)
            return carry

        def left(m, carry):
            ship(LEFT, m)
            return carry

        def keep_all(j, carry):
            collect(k, j)
            return carry

        @pl.when(c == 0)
        def _():
            lax.fori_loop(0, n_col - 1, right, 0)
            collect(k, c)

        @pl.when(c == n_col - 1)
        def _():
            lax.fori_loop(0, n_col - 1, left, 0)
            collect(k, c)

        @pl.when((c > 0) & (c < n_col - 1))
        def _():
            lax.fori_loop(0, n_col, keep_all, 0)

    def scatter_middle(k):
        p = parts[k]

        def unit(n, carry):
            right = n - c
            left = n - (n_col - 1 - c)

            def through(way, j, s):
                pl.when(s == 0)(lambda: announce(way, k, j, True))
                forward(way, k, j, s, True)

            @pl.when((c > 0) & (right >= 0) & (right < (n_col - 1 - c) * p))
            def _():
                through(RIGHT, n_col - 1 - right // p, right % p)

            @pl.when((c < n_col - 1) & (left >= 0) & (left < c * p))
            def _():
                through(LEFT, left // p, left % p)

            return carry

        lax.fori_loop(1, (n_col - 2) * p + 1, unit, 0)

    def finish(k):
        first, columns = pieces[k]
        tile, offset = first // LANES, first % LANES
        width = shard // parts[k]
        d = depth[k]

        def write(ways):
            for way in ways:
                scale(way, k, c).wait_recv()

            def part(s, carry):
                for way in ways:
                    message(way, k, c, s).wait_recv()

                def one(b):
                    x = rows[k][c * shard + s * width + b]
                    for way in ways:
                        x = x + received(way, k, c, s, b)
                    turned = [pltpu.roll(x, (offset - m * columns) % LANES, 1) for m in range(fold[k])]
                    return [y[:, offset:offset + columns].astype(out.dtype) for y in turned]

                for b, pieces_of in [(b, one(b)) for b in range(width)]:
                    for m, y in enumerate(pieces_of):
                        out[s * width + b, pl.ds(m * d, d), pl.ds(first, columns)] = y
                return carry

            lax.fori_loop(0, parts[k], part, 0)

        pl.when(c == 0)(lambda: write((LEFT,)))
        pl.when(c == n_col - 1)(lambda: write((RIGHT,)))
        pl.when((c > 0) & (c < n_col - 1))(lambda: write((RIGHT, LEFT)))

    own[0].wait()
    pack_own(0)
    for copy in tables:
        copy.wait()
    ends = jnp.where(c > 0, 1, 0) + jnp.where(c < n_col - 1, 1, 0)
    pl.semaphore_wait(barrier, len(direct) + 1 + ends)
    gather_start(0)
    for copy in own[1:]:
        copy.wait()
    pack_own(1)
    mark_rows()
    gather_relay(0)
    gather_start(1)
    for k in range(2, chunks):
        pack_own(k)
    fetch.wait()
    gather_finish(0)

    def advance(k):
        if k + 1 < chunks:
            gather_relay(k + 1)
        if k + 2 < chunks:
            gather_start(k + 2)

    for k in range(chunks):
        compute(k, (lambda: advance(0)) if k == 0 else None)
        scatter_start(k)
        if k > 0:
            advance(k)
        if k > 1:
            finish(k - 2)
        if k > 0:
            scatter_middle(k - 1)
        if k + 1 < chunks:
            gather_finish(k + 1)
    finish(chunks - 2)
    scatter_middle(chunks - 1)
    finish(chunks - 1)

    for k in range(chunks):
        gathered(k, n_chips - 1, ag_send).wait_send()
        gathered(k, n_chips, pair_send).wait_send()
        shards = pl.ds(0, n_col - 1)
        remote(send_q[k].at[shards], recv_q[k].at[shards], rs_send.at[k], rs_recv[k].at[0, 0],
               row=partner).wait_send()
        remote(send_s[k].at[shards], recv_s[k].at[shards], sc_send.at[k], sc_recv.at[k, 0],
               row=partner).wait_send()


def local(n_row, n_col, features, block_values, row_ptr, block_cols):
    slots, block = block_values.shape[2], block_values.shape[3]
    live = slots * 3 // 4
    own_blocks = features.shape[0] // block
    group_blocks = own_blocks * n_row
    columns = features.shape[1]
    pieces = column_chunks(columns)
    shard = (row_ptr.shape[2] - 1) // n_col
    parts = [parts_of(width, shard) for _, width in pieces]
    depth = [block * width // LANES for _, width in pieces]
    hbm = pl.BlockSpec(memory_space=pltpu.HBM)
    halves = 2 if n_row == 8 else 1
    gathers = (len(pieces), n_row // 2, halves)

    def per_chunk(make):
        return [make(p, d) for p, d in zip(parts, depth)]

    dma = pltpu.SemaphoreType.DMA
    result = pl.pallas_call(
        functools.partial(kernel, n_row, n_col, pieces),
        out_shape=jax.ShapeDtypeStruct((shard, block, columns), jnp.bfloat16),
        in_specs=[hbm] * 4,
        out_specs=pl.BlockSpec(memory_space=pltpu.VMEM),
        scratch_shapes=[
            pltpu.SMEM(row_ptr.shape, row_ptr.dtype),
            pltpu.SMEM(block_cols.shape, block_cols.dtype),
            pltpu.VMEM((columns // LANES, own_blocks, block, LANES), jnp.bfloat16),
            per_chunk(lambda p, d: pltpu.VMEM((group_blocks, d, LANES), jnp.bfloat16)),
            pltpu.VMEM((live, block, block), jnp.bfloat16),
            pltpu.VMEM((live, LANES), jnp.float32),
            pltpu.VMEM((live, block, LANES), jnp.float32),
            per_chunk(lambda p, d: pltpu.VMEM((shard * n_col, d, LANES), jnp.float32)),
            per_chunk(lambda p, d: pltpu.VMEM((n_col, 1, LANES), jnp.float32)),
            per_chunk(lambda p, d: pltpu.VMEM((n_col, shard, d, LANES), jnp.int16)),
            per_chunk(lambda p, d: pltpu.VMEM((n_col + 1, shard, d, LANES), jnp.int16)),
            per_chunk(lambda p, d: pltpu.VMEM((n_col, 1, LANES), jnp.float32)),
            per_chunk(lambda p, d: pltpu.VMEM((n_col + 1, 1, LANES), jnp.float32)),
            dma((columns // LANES + 1,)),
            dma((2,)),
            dma((len(pieces),)),
            dma(gathers),
            dma((len(pieces),)),
            dma((len(pieces),)),
            dma((len(pieces),)),
            per_chunk(lambda p, d: dma((n_col + 1, p))),
            dma((len(pieces),)),
            dma((len(pieces), n_col + 1)),
        ],
        compiler_params=pltpu.CompilerParams(
            collective_id=0, has_side_effects=True, vmem_limit_bytes=60000000
        ),
    )(row_ptr, block_cols, features.reshape(own_blocks, block, -1), block_values)
    return result.reshape(shard * block, -1)


def solution(mesh):
    return jax.shard_map(
        functools.partial(local, mesh.shape["row"], mesh.shape["col"]),
        mesh=mesh,
        in_specs=(
            P(("col", "row"), None),
            P("row", "col", None, None, None),
            P("row", "col", None),
            P("row", "col", None),
        ),
        out_specs=P(("row", "col"), None),
        check_vma=False,
    )
```

time: 149 us -> 96.3 us (0.65)
  Pallas kernels: 146 us -> 92.3 us
    pallas_call x1, Pallas kernels: 146 us -> 92.3 us  [local(): pl.pallas_call(functools.partial(kernel, n_row, n_col, pieces), out_shape...]
where the time goes in v2:
time: 96.3 us; the launch traced here: 94.6 us
  Pallas kernels  92.3 us (96%)
  local copies, waits for them, and re-layouts  2.26 us (2%)
    pallas_call x1, Pallas kernels, local(): pl.pallas_call(functools.partial(kernel, n_row, n_col, pieces), out_shape...  92.3 us
    unnamed x1, local copies, waits for them, and re-layouts  2.26 us

profile of v2, /device:TPU:8, one launch (start us, length us, event | category | flops | bytes accessed | tf_op | source)
XLA Modules:
  0.0 94.6 jit_solution(10711569389784739191)
XLA Ops:
  0.0 92.3 %shard_map.46 = bf16[16,128,256]{2,1,0:T(8,128)(2,1)} custom-call(s32[1,1,65]{2,1,0:T(1,128)} %pointers_hbm.1, s32[1,1,192]{2,1,0:T(1,128)} %block_cols_hbm.1, bf16[16,128,256]{2,1,0:T(8,128)(2,1)} %bitcast.3, bf16[1,1,192,128,128]{4,3,2,1,0:T(8,128)(2,1)} %values_hbm.1), custom_call_target="tpu_custom_call" | custom-call | tf_op jit(solution)/shard_map/pallas_call | solution.py:464
  92.3 2.3 %copy.6 = bf16[2048,256]{1,0:T(8,128)(2,1)} copy(bf16[2048,256]{1,0:T(8,128)(2,1)} %bitcast.2) | data formatting | bytes 2097152

commit v3 on v2

--- a/solution.py
+++ b/solution.py
@@ -362,6 +362,31 @@
 
         lax.fori_loop(1, (n_col - 2) * p + 1, unit, 0)
 
+    def scatter_hop(k, hop):
+        p = parts[k]
+
+        def through(way, j, s):
+            pl.when(s == 0)(lambda: announce(way, k, j, True))
+            forward(way, k, j, s, True)
+
+        def right(m, carry):
+            through(RIGHT, n_col - 1 - m // p, m % p)
+            return carry
+
+        def left(m, carry):
+            through(LEFT, m // p, m % p)
+            return carry
+
+        total = (n_col - 1 - hop) * p
+
+        @pl.when(c == hop)
+        def _():
+            lax.fori_loop(0, total, right, 0)
+
+        @pl.when(n_col - 1 - c == hop)
+        def _():
+            lax.fori_loop(0, total, left, 0)
+
     def finish(k):
         first, columns = pieces[k]
         tile, offset = first // LANES, first % LANES
@@ -412,6 +437,13 @@
     fetch.wait()
     gather_finish(0)
 
+    def scatter_on(k):
+        for hop in range(1, n_col - 1):
+            if 0 <= k - hop < chunks - 1:
+                scatter_hop(k - hop, hop)
+        if 0 <= k - (n_col - 1) < chunks - 1:
+            finish(k - (n_col - 1))
+
     def advance(k):
         if k + 1 < chunks:
             gather_relay(k + 1)
@@ -423,13 +455,11 @@
         scatter_start(k)
         if k > 0:
             advance(k)
-        if k > 1:
-            finish(k - 2)
-        if k > 0:
-            scatter_middle(k - 1)
+        scatter_on(k)
         if k + 1 < chunks:
             gather_finish(k + 1)
-    finish(chunks - 2)
+    for k in range(chunks, chunks + n_col - 2):
+        scatter_on(k)
     scatter_middle(chunks - 1)
     finish(chunks - 1)
 
@@ -492,9 +522,12 @@
             dma((len(pieces), n_col + 1)),
         ],
         compiler_params=pltpu.CompilerParams(
-            collective_id=0, has_side_effects=True, vmem_limit_bytes=60000000
+            collective_id=0, has_side_effects=True, vmem_limit_bytes=50000000
         ),
-    )(row_ptr, block_cols, features.reshape(own_blocks, block, -1), block_values)
+    )(*[
+        pltpu.with_memory_space_constraint(x, pltpu.HBM)
+        for x in (row_ptr, block_cols, features.reshape(own_blocks, block, -1), block_values)
+    ])
     return result.reshape(shard * block, -1)
 
 

time: 96.3 us -> 88.6 us (0.920)
  Pallas kernels: 92.3 us -> 86 us
  local copies, waits for them, and re-layouts: 2.26 us -> 0.97 us
    pallas_call x1, Pallas kernels: 92.3 us -> 86 us  [local(): pl.pallas_call(functools.partial(kernel, n_row, n_col, pieces), out_shape...]
    unnamed x1, local copies, waits for them, and re-layouts: 2.26 us -> 0.97 us
where the time goes in v3:
time: 88.6 us; the launch traced here: 87 us
  Pallas kernels  86 us (97%)
  local copies, waits for them, and re-layouts  0.97 us (1%)
    pallas_call x1, Pallas kernels, local(): pl.pallas_call(functools.partial(kernel, n_row, n_col, pieces), out_shape...  86 us

profile of v3, /device:TPU:8, one launch (start us, length us, event | category | flops | bytes accessed | tf_op | source)
XLA Modules:
  0.0 87.0 jit_solution(2677559603262791681)
XLA Ops:
  0.0 86.0 %shard_map.46 = bf16[16,128,256]{2,1,0:T(8,128)(2,1)S(1)} custom-call(s32[1,1,65]{2,1,0:T(1,128)} %pointers_hbm.1, s32[1,1,192]{2,1,0:T(1,128)} %block_cols_hbm.1, bf16[16,128,256]{2,1,0:T(8,128)(2,1)} %bitcast.3, bf16[1,1,192,128,128]{4,3,2,1,0:T(8,128)(2,1)} %values_hbm.1), custom_call_target="tpu_custom_call" | custom-call | tf_op jit(solution)/shard_map/pallas_call | solution.py:494
  86.0 1.0 %copy.6 = bf16[2048,256]{1,0:T(8,128)(2,1)} copy(bf16[2048,256]{1,0:T(8,128)(2,1)S(1)} %bitcast.2) | data formatting | bytes 2097152

commit v4 on v3

--- a/solution.py
+++ b/solution.py
@@ -59,7 +59,7 @@
         return chip_to(o) if square else (chip + n_chips - o) % n_chips
 
     partner = chip * 2 + 1 - core
-    direct = (1, 2) if square else tuple(range(1, n_chips))
+    others = (1, 2) if square else tuple(range(1, n_chips))
 
     def slot(k, row, h):
         return panels[k].at[pl.ds(row * own_blocks + h * half, half)]
@@ -90,7 +90,7 @@
             barrier, inc=1, device_id=where, device_id_type=pl.DeviceIdType.MESH
         )
 
-    for o in direct:
+    for o in others:
         greet(row=chip_to(o) * 2 + core)
     greet(row=partner)
     pl.when(c > 0)(lambda: greet(col=c - 1))
@@ -136,7 +136,7 @@
     def piece(k, o, h, source, to):
         return remote(
             slot(k, source * 2 + core, h), slot(k, source * 2 + core, h),
-            ag_send.at[k], ag_recv.at[k, o, h], row=to * 2 + core,
+            ag_send.at[k], ag_recv.at[k, o - 1, h], row=to * 2 + core,
         )
 
     def across(k, o, h):
@@ -159,21 +159,30 @@
         return remote(span, span, sent.at[k], pair_recv.at[k], row=partner)
 
     if square:
-        order = ((1, 0), (2, 1), (1, 1), (2, 0))
+        early, late = ((1, 0), (2, 1)), ((1, 1), (2, 0))
     else:
-        order = tuple((o, 0) for o in direct)
-
-    def gather_start(k):
-        for o, h in order:
+        early, late = tuple((o, 0) for o in others), ()
+
+    def gather_early(k):
+        for o, h in early:
+            across(k, o, h).start()
+
+    def gather_late(k):
+        for o, h in late:
             across(k, o, h).start()
         for h in range(halves):
             pair(k, 0, h, core).start()
 
     def gather_relay(k):
-        for o, h in order:
+        for o, h in early:
             arriving(k, o, h).wait_recv()
-            if square and (o, h) in ((1, 0), (2, 1)):
+            if square:
                 relay(k, h).start()
+            pair(k, o, h, core).start()
+
+    def gather_pass(k):
+        for o, h in late:
+            arriving(k, o, h).wait_recv()
             pair(k, o, h, core).start()
 
     def gather_finish(k):
@@ -184,7 +193,7 @@
         gathered(k, n_chips, pair_send).wait_recv()
 
     unroll = 1
-    for u in (2, 4, 8, 16):
+    for u in (2, 4, 8, 16, 48):
         if live % u == 0:
             unroll = u
 
@@ -424,37 +433,45 @@
     for copy in tables:
         copy.wait()
     ends = jnp.where(c > 0, 1, 0) + jnp.where(c < n_col - 1, 1, 0)
-    pl.semaphore_wait(barrier, len(direct) + 1 + ends)
-    gather_start(0)
+    pl.semaphore_wait(barrier, len(others) + 1 + ends)
+    gather_early(0)
+    gather_late(0)
     for copy in own[1:]:
         copy.wait()
     pack_own(1)
+    gather_early(1)
+    gather_relay(0)
+    gather_late(1)
     mark_rows()
-    gather_relay(0)
-    gather_start(1)
     for k in range(2, chunks):
         pack_own(k)
+    gather_pass(0)
     fetch.wait()
     gather_finish(0)
 
     def scatter_on(k):
-        for hop in range(1, n_col - 1):
+        if 0 <= k - (n_col - 1) < chunks - 1:
+            finish(k - (n_col - 1))
+        for hop in range(n_col - 2, 0, -1):
             if 0 <= k - hop < chunks - 1:
                 scatter_hop(k - hop, hop)
-        if 0 <= k - (n_col - 1) < chunks - 1:
-            finish(k - (n_col - 1))
 
     def advance(k):
         if k + 1 < chunks:
             gather_relay(k + 1)
         if k + 2 < chunks:
-            gather_start(k + 2)
-
+            gather_early(k + 2)
+            gather_late(k + 2)
+
+    advance(0)
     for k in range(chunks):
-        compute(k, (lambda: advance(0)) if k == 0 else None)
+        if k == 0:
+            compute(k)
+        else:
+            compute(k, lambda: advance(k))
         scatter_start(k)
-        if k > 0:
-            advance(k)
+        if k < chunks - 1:
+            gather_pass(k + 1)
         scatter_on(k)
         if k + 1 < chunks:
             gather_finish(k + 1)
@@ -482,10 +499,11 @@
     pieces = column_chunks(columns)
     shard = (row_ptr.shape[2] - 1) // n_col
     parts = [parts_of(width, shard) for _, width in pieces]
+    parts[-1] = parts_of(LANES, shard)
     depth = [block * width // LANES for _, width in pieces]
     hbm = pl.BlockSpec(memory_space=pltpu.HBM)
     halves = 2 if n_row == 8 else 1
-    gathers = (len(pieces), n_row // 2, halves)
+    gathers = (len(pieces), max(n_row // 2 - 1, 1), halves)
 
     def per_chunk(make):
         return [make(p, d) for p, d in zip(parts, depth)]

time: 88.6 us -> 86.6 us (0.977); the launches traced: 87 us -> 86.4 us
  no operation moved by 1% of the time
where the time goes in v4:
time: 86.6 us; the launch traced here: 86.4 us
  Pallas kernels  85.5 us (99%)
  local copies, waits for them, and re-layouts  0.97 us (1%)
    pallas_call x1, Pallas kernels, local(): pl.pallas_call(functools.partial(kernel, n_row, n_col, pieces), out_shape...  85.5 us

profile of v4, /device:TPU:8, one launch (start us, length us, event | category | flops | bytes accessed | tf_op | source)
XLA Modules:
  0.0 86.4 jit_solution(16835103387199766509)
XLA Ops:
  0.0 85.5 %shard_map.46 = bf16[16,128,256]{2,1,0:T(8,128)(2,1)S(1)} custom-call(s32[1,1,65]{2,1,0:T(1,128)} %pointers_hbm.1, s32[1,1,192]{2,1,0:T(1,128)} %block_cols_hbm.1, bf16[16,128,256]{2,1,0:T(8,128)(2,1)} %bitcast.3, bf16[1,1,192,128,128]{4,3,2,1,0:T(8,128)(2,1)} %values_hbm.1), custom_call_target="tpu_custom_call" | custom-call | tf_op jit(solution)/shard_map/pallas_call | solution.py:512
  85.5 1.0 %copy.6 = bf16[2048,256]{1,0:T(8,128)(2,1)} copy(bf16[2048,256]{1,0:T(8,128)(2,1)S(1)} %bitcast.2) | data formatting | bytes 2097152
